TPU v7x, 32 devices: a whole 2x2x4 slice. The times are simulated.
32 devices in a mesh: dp: 8 (over z, y), tensor: 4 (over x, core).
Axes of the slice: x: 2, y: 2, z: 4, core: 2. Of those that a mesh axis runs over, the one named last changes fastest.
Arguments:
- acts: bfloat16 [8, 2048, 1024], P('dp', 'tensor'), may hold values from -6 to 6
- grad_out: bfloat16 [8, 2048, 1024], P('dp', 'tensor'), may hold values from -6 to 6
- norm_gain: float32 [1024], replicated, may hold values from 0.5 to 1.5
- w_zx: bfloat16 [1024, 2, 2048], P('dp', None, 'tensor'), may hold values from -0.1875 to 0.1875
- w_bc: bfloat16 [1024, 256], P('dp'), may hold values from -0.1875 to 0.1875
- w_dt: bfloat16 [1024, 32], P('dp', 'tensor'), may hold values from -0.1875 to 0.1875
- w_out: bfloat16 [1024, 2048], P('dp', 'tensor'), may hold values from -0.125 to 0.125
- conv_x: float32 [4, 2048], replicated, may hold values from -3 to 3
- conv_x_bias: float32 [2048], replicated, may hold values from -0.5 to 0.5
- conv_bc: float32 [4, 256], replicated, may hold values from -3 to 3
- conv_bc_bias: float32 [256], replicated, may hold values from -0.5 to 0.5
- dt_bias: float32 [32], replicated, may hold values from -7 to -2
- a_log: float32 [32], replicated, may hold values from 0 to 2.77
- d_skip: float32 [32], replicated, may hold values from 0.5 to 1.5
- gate_gain: float32 [2048], replicated, may hold values from 0.5 to 1.5
Outputs:
- out_acts: bfloat16 [8, 2048, 1024], P('dp', 'tensor')
- grad_acts: float32 [8, 2048, 1024], P('dp', 'tensor')
- grad_norm_gain: float32 [1024], replicated
- grad_w_zx: float32 [1024, 2, 2048], P('dp', None, 'tensor')
- grad_w_bc: float32 [1024, 256], P('dp')
- grad_w_dt: float32 [1024, 32], P('dp', 'tensor')
- grad_w_out: float32 [1024, 2048], P('dp', 'tensor')
- grad_conv_x: float32 [4, 2048], replicated
- grad_conv_x_bias: float32 [2048], replicated
- grad_conv_bc: float32 [4, 256], replicated
- grad_conv_bc_bias: float32 [256], replicated
- grad_dt_bias: float32 [32], replicated
- grad_a_log: float32 [32], replicated
- grad_d_skip: float32 [32], replicated
- grad_gate_gain: float32 [2048], replicated
All inputs are finite; a program needn't handle non-finite values.
Results may differ from a plain program's by a relative error of at most 0.0096.
Values may be sent and summed in bfloat16 or wider, within the bound.
A program may use at most 192 MiB of HBM per device.

v0:
```python
import jax
import jax.numpy as jnp
from jax import lax
from jax.sharding import PartitionSpec as P

BLOCK_LEN = 256
EPSILON = 1e-05
FULL_PRECISION = lax.Precision.HIGHEST
CONTRACT_LAST = (((1,), (1,)), ((), ()))
CONTRACT_FIRST = (((0,), (0,)), ((), ()))


def causal_conv(values, conv_taps):
    tap_count = conv_taps.shape[0]
    length = values.shape[0]
    padded = jnp.pad(values, ((tap_count - 1, 0), (0, 0)))
    result = conv_taps[0] * padded[0:length]
    for offset in range(1, tap_count):
        result = result + conv_taps[offset] * padded[offset : offset + length]
    return result


def ssd_scan(x_heads, step_dt, decay_rate, b_mat, c_mat, block_size):
    length, head_count, head_width = x_heads.shape
    state_count = b_mat.shape[1]
    block_count = length // block_size
    x_blocks = x_heads.reshape(block_count, block_size, head_count, head_width)
    dt_blocks = step_dt.reshape(block_count, block_size, head_count)
    b_blocks = b_mat.reshape(block_count, block_size, state_count)
    c_blocks = c_mat.reshape(block_count, block_size, state_count)
    positions = jnp.arange(block_size)
    causal_mask = (positions[:, None] >= positions[None, :]).astype(jnp.float32)

    def step_block(state, inputs):
        x_block, dt_block, b_block, c_block = inputs
        cum_logs = jnp.cumsum(dt_block * decay_rate[None, :], axis=0)
        scores = jnp.dot(c_block, b_block.T, precision=FULL_PRECISION)
        log_gaps = (cum_logs[:, None, :] - cum_logs[None, :, :]) * causal_mask[:, :, None]
        weights = (
            scores[:, :, None] * jnp.exp(log_gaps) * causal_mask[:, :, None] * dt_block[None, :, :]
        )
        within = jnp.einsum("ijh,jhp->ihp", weights, x_block, precision=FULL_PRECISION)
        carried = (
            jnp.einsum("in,hpn->ihp", c_block, state, precision=FULL_PRECISION)
            * jnp.exp(cum_logs)[:, :, None]
        )
        block_total = cum_logs[-1]
        state_weight = jnp.exp(block_total[None, :] - cum_logs) * dt_block
        update = jnp.einsum(
            "jhp,jn->hpn", x_block * state_weight[:, :, None], b_block, precision=FULL_PRECISION
        )
        new_state = state * jnp.exp(block_total)[:, None, None] + update
        return (new_state, within + carried)

    zero_state = jnp.zeros((head_count, head_width, state_count), jnp.float32)
    final_state, outputs = lax.scan(
        jax.checkpoint(step_block), zero_state, (x_blocks, dt_blocks, b_blocks, c_blocks)
    )
    return outputs.reshape(length, head_count, head_width)


def pre_norm(acts_row, norm_gain):
    return (
        acts_row
        * lax.rsqrt(jnp.mean(acts_row * acts_row, axis=-1, keepdims=True) + EPSILON)
        * norm_gain
    )


def conv_part(x_vals, bc_vals, x_taps, x_shift, bc_taps, bc_shift):
    x_conv = jax.nn.silu(causal_conv(x_vals, x_taps) + x_shift)
    bc_conv = jax.nn.silu(causal_conv(bc_vals, bc_taps) + bc_shift)
    return (x_conv, bc_conv)


def mix_part(x_vals, b_vals, c_vals, dt_vals, dt_shift, log_rate, skip_gain, gate_vals):
    length = x_vals.shape[0]
    head_count = dt_vals.shape[1]
    x_heads = x_vals.reshape(length, head_count, -1)
    step_dt = jax.nn.softplus(dt_vals + dt_shift)
    mixed = (
        ssd_scan(x_heads, step_dt, -jnp.exp(log_rate), b_vals, c_vals, BLOCK_LEN)
        + skip_gain[None, :, None] * x_heads
    )
    return mixed.reshape(length, -1) * jax.nn.silu(gate_vals)


def widen(piece, start, full_size):
    holder = jnp.zeros(piece.shape[:-1] + (full_size,), jnp.float32)
    return lax.dynamic_update_slice_in_dim(holder, piece, start, piece.ndim - 1)


def body(
    acts,
    grad_out,
    norm_gain,
    w_zx,
    w_bc,
    w_dt,
    w_out,
    conv_x,
    conv_x_bias,
    conv_bc,
    conv_bc_bias,
    dt_bias,
    a_log,
    d_skip,
    gate_gain,
):
    parts = lax.axis_size("tensor")
    rank = lax.axis_index("tensor")
    local_rows = acts.shape[1]
    channels = w_zx.shape[2]
    head_count = w_dt.shape[1]
    state_count = w_bc.shape[1] // 2
    total_channels = channels * parts
    total_heads = head_count * parts
    chan_start = rank * channels
    head_start = rank * head_count
    zx_full, bc_full, dt_full, out_full = (
        lax.all_gather(w_zx, "dp", axis=0, tiled=True),
        lax.all_gather(w_bc, "dp", axis=0, tiled=True),
        lax.all_gather(w_dt, "dp", axis=0, tiled=True),
        lax.all_gather(w_out, "dp", axis=0, tiled=True),
    )
    acts_row = acts[0].astype(jnp.float32)
    normed_in, pre_back = jax.vjp(pre_norm, acts_row, norm_gain)
    hidden = lax.all_gather(normed_in.astype(jnp.bfloat16), "tensor", axis=0, tiled=True)
    zx_proj = jnp.einsum("ld,dkc->lkc", hidden, zx_full, preferred_element_type=jnp.float32)
    bc_proj = jnp.dot(hidden, bc_full, preferred_element_type=jnp.float32)
    dt_proj = jnp.dot(hidden, dt_full, preferred_element_type=jnp.float32)
    conv_x_local = lax.dynamic_slice_in_dim(conv_x, chan_start, channels, 1)
    conv_xb_local = lax.dynamic_slice_in_dim(conv_x_bias, chan_start, channels, 0)
    dt_bias_local = lax.dynamic_slice_in_dim(dt_bias, head_start, head_count, 0)
    a_log_local = lax.dynamic_slice_in_dim(a_log, head_start, head_count, 0)
    d_skip_local = lax.dynamic_slice_in_dim(d_skip, head_start, head_count, 0)
    gain_local = lax.dynamic_slice_in_dim(gate_gain, chan_start, channels, 0)
    conv_outs, conv_back = jax.vjp(
        conv_part, zx_proj[:, 1], bc_proj, conv_x_local, conv_xb_local, conv_bc, conv_bc_bias
    )
    x_conv, bc_conv = conv_outs
    x_low = x_conv.astype(jnp.bfloat16)
    b_low = bc_conv[:, :state_count].astype(jnp.bfloat16)
    c_low = bc_conv[:, state_count:].astype(jnp.bfloat16)
    gated, mix_back = jax.vjp(
        mix_part,
        x_low.astype(jnp.float32),
        b_low.astype(jnp.float32),
        c_low.astype(jnp.float32),
        dt_proj,
        dt_bias_local,
        a_log_local,
        d_skip_local,
        zx_proj[:, 0],
    )
    square_total = lax.psum(jnp.sum(gated * gated, axis=1), "tensor")
    inv_rms = lax.rsqrt(square_total / total_channels + EPSILON)[:, None]
    mixed_out = (gated * inv_rms * gain_local).astype(jnp.bfloat16)
    projected = lax.psum_scatter(
        lax.dot_general(mixed_out, out_full, CONTRACT_LAST, preferred_element_type=jnp.float32),
        "tensor",
        scatter_dimension=0,
        tiled=True,
    )
    out_acts = (acts_row + projected).astype(jnp.bfloat16)[None]
    grad_row = grad_out[0]
    grad_rows_all = lax.all_gather(grad_row, "tensor", axis=0, tiled=True)
    grad_mixed = jnp.dot(grad_rows_all, out_full, preferred_element_type=jnp.float32).astype(
        jnp.bfloat16
    )
    grad_out_w = lax.dot_general(
        grad_rows_all, mixed_out, CONTRACT_FIRST, preferred_element_type=jnp.float32
    )
    grad_normed = grad_mixed.astype(jnp.float32)
    grad_gain_local = jnp.sum(grad_normed * gated * inv_rms, axis=0)
    scaled = grad_normed * gain_local
    row_dot = lax.psum(jnp.sum(scaled * gated, axis=1), "tensor")
    grad_gated = (
        inv_rms * scaled
        - gated * (inv_rms * inv_rms * inv_rms) * (row_dot / total_channels)[:, None]
    )
    (
        grad_x_low,
        grad_b,
        grad_c,
        grad_dt_in,
        grad_dt_shift,
        grad_log_rate,
        grad_skip,
        grad_gate_in,
    ) = mix_back(grad_gated)
    grad_x_in, grad_bc_part, grad_x_taps, grad_x_shift, grad_bc_taps, grad_bc_shift = conv_back(
        (grad_x_low, jnp.concatenate([grad_b, grad_c], axis=1))
    )
    grad_bc_in = lax.psum(grad_bc_part, "tensor").astype(jnp.bfloat16)
    grad_zx = jnp.stack([grad_gate_in.astype(jnp.bfloat16), grad_x_in.astype(jnp.bfloat16)], axis=1)
    grad_dt_low = grad_dt_in.astype(jnp.bfloat16)
    grad_zx_w = jnp.einsum("ld,lkc->dkc", hidden, grad_zx, preferred_element_type=jnp.float32)
    grad_bc_w = lax.dot_general(
        hidden, grad_bc_in, CONTRACT_FIRST, preferred_element_type=jnp.float32
    )
    grad_dt_w = lax.dot_general(
        hidden, grad_dt_low, CONTRACT_FIRST, preferred_element_type=jnp.float32
    )
    from_zx = jnp.einsum("lkc,dkc->ld", grad_zx, zx_full, preferred_element_type=jnp.float32)
    grad_hidden = lax.psum_scatter(
        from_zx
        + lax.dot_general(grad_dt_low, dt_full, CONTRACT_LAST, preferred_element_type=jnp.float32),
        "tensor",
        scatter_dimension=0,
        tiled=True,
    )
    bc_piece = lax.dynamic_slice_in_dim(grad_bc_in, rank * local_rows, local_rows, 0)
    grad_hidden = grad_hidden + lax.dot_general(
        bc_piece, bc_full, CONTRACT_LAST, preferred_element_type=jnp.float32
    )
    grad_acts_norm, grad_norm_gain = pre_back(grad_hidden)
    grad_acts = (grad_row.astype(jnp.float32) + grad_acts_norm)[None]
    grad_w_zx, grad_w_bc, grad_w_dt, grad_w_out = (
        lax.psum_scatter(grad_zx_w, "dp", scatter_dimension=0, tiled=True),
        lax.psum_scatter(grad_bc_w, "dp", scatter_dimension=0, tiled=True),
        lax.psum_scatter(grad_dt_w, "dp", scatter_dimension=0, tiled=True),
        lax.psum_scatter(grad_out_w, "dp", scatter_dimension=0, tiled=True),
    )
    small_sums = lax.psum(
        (
            grad_norm_gain,
            widen(grad_x_taps, chan_start, total_channels),
            widen(grad_x_shift, chan_start, total_channels),
            grad_bc_taps,
            grad_bc_shift,
            widen(grad_dt_shift, head_start, total_heads),
            widen(grad_log_rate, head_start, total_heads),
            widen(grad_skip, head_start, total_heads),
            widen(grad_gain_local, chan_start, total_channels),
        ),
        ("dp", "tensor"),
    )
    grad_ng, grad_cx, grad_cxb, grad_cbc, grad_cbcb, grad_dtb, grad_alog, grad_dsk, grad_gg = (
        small_sums
    )
    return (
        out_acts,
        grad_acts,
        grad_ng,
        grad_w_zx,
        grad_w_bc,
        grad_w_dt,
        grad_w_out,
        grad_cx,
        grad_cxb,
        grad_cbc,
        grad_cbcb,
        grad_dtb,
        grad_alog,
        grad_dsk,
        grad_gg,
    )


def solution(mesh):
    in_specs = (
        P("dp", "tensor", None),
        P("dp", "tensor", None),
        P(),
        P("dp", None, "tensor"),
        P("dp", None),
        P("dp", "tensor"),
        P("dp", "tensor"),
        P(),
        P(),
        P(),
        P(),
        P(),
        P(),
        P(),
        P(),
    )
    out_specs = (
        P("dp", "tensor", None),
        P("dp", "tensor", None),
        P(),
        P("dp", None, "tensor"),
        P("dp", None),
        P("dp", "tensor"),
        P("dp", "tensor"),
        P(),
        P(),
        P(),
        P(),
        P(),
        P(),
        P(),
        P(),
    )
    return jax.shard_map(body, mesh=mesh, in_specs=in_specs, out_specs=out_specs, check_vma=False)
```

profile of v0, /device:TPU:0, one launch (start us, length us, event | category | flops | bytes accessed | tf_op | source)
XLA Modules:
  0.0 918.6 jit_solution(7278153467009917441)
XLA Ops:
  16.2 27.9 %all_gather.19 = bf16[1024,8]{0,1:T(8,128)(2,1)S(1)} all-gather(bf16[128,8]{0,1:T(8,128)(2,1)S(1)} %copy-done.49), channel_id=1, replica_groups=mesh['dp'=8,'tensor'=4] {'dp'}, dimensions={0}, use_global_device_ids=true | all-gather | bytes 18432 | tf_op jit(solution)/shard_map/all_gather | solution.py:123
  44.2 32.4 %all_gather.21 = bf16[1024,256]{1,0:T(8,128)(2,1)S(1)} all-gather(bf16[128,256]{1,0:T(8,128)(2,1)S(1)} %copy-done.20), channel_id=1, replica_groups=mesh['dp'=8,'tensor'=4] {'dp'}, dimensions={0}, use_global_device_ids=true | all-gather | bytes 589824 | tf_op jit(solution)/shard_map/all_gather | solution.py:122
  77.6 3.8 fusion.161
  86.3 15.2 %all-gather.8.cloned.1.call-done = bf16[1024,2,512]{2,0,1:T(8,128)(2,1)} async-done(((bf16[128,2,512]{2,0,1:T(8,128)(2,1)}), bf16[1024,2,512]{2,0,1:T(8,128)(2,1)}) %all-gather.8.cloned.1.call-update) | async-done | bytes 2097168 | tf_op jit(solution)/shard_map/all_gather | solution.py:121
  101.5 7.1 fusion.109
  112.3 4.7 fusion.123
  117.0 7.1 reshape.372
  124.1 6.9 copy.89
  130.9 4.0 compare_select_fusion.2
  137.4 87.5 %while.43 = (s32[]{:T(128)}, f32[8,64,128]{2,1,0:T(8,128)S(1)}, f32[8,256,8,64]{1,3,2,0:T(8,128)}, f32[8,8,64,128]{3,2,1,0:T(8,128)}, f32[8,256,8]{1,2,0:T(8,128...) while((s32[]{:T(128)}, f32[8,64,128]{2,1,0:T(8,128)S(1)}, ...), condition=%wide.region_4.5_spmd.clone.clone, body=%wide.region_1.4_spmd.clone.clone.sunk | while | flops 909711360 | bytes 5641051 | solution.py:56
  140.0 3.6 fusion.270
  150.9 3.6 fusion.270
  161.9 3.6 fusion.270
  172.9 3.6 fusion.270
  183.8 3.6 fusion.270
  194.7 3.6 fusion.270
  205.7 3.6 fusion.270
  216.6 3.6 fusion.270
  225.0 6.9 copy.101
  231.9 7.5 reshape.369
  239.4 7.6 multiply_reduce_fusion.8
  246.9 5.7 psum.84
  252.7 7.2 fusion.130
  260.0 7.4 fusion.96
  267.5 6.8 psum.85
  274.3 11.7 %multiply_reduce_fusion.3 = (f32[512]{0:T(512)}, f32[2048,512]{1,0:T(8,128)}, bf16[2048,1,512]{2,0,1:T(8,128)(2,1)}) fusion(f32[2048,512]{1,0:T(8,128)} %get-tuple-element.766, f32[2048,2,512]{2,0,1:T(8,128)} %copy-done.1, f32[2048]{0:T(1024)S(1)} %broadcast_multiply_fusion.8, f32[2048,512]{1,0:T(8,128)} %get-tuple-element.762, ...), kind=kLoop, calls=%fused_computation.161 | loop fusion | flops 30408192 | bytes 25196544 | tf_op jit(solution)/shard_map/transpose(jvp())/reduce_sum | solution.py:83
  286.0 7.1 reshape.370
  293.1 6.8 copy.94
  305.2 198.0 %while.42 = (s32[]{:T(128)}, f32[8]{0:T(128)}, f32[8,64,128]{2,1,0:T(8,128)S(1)}, f32[8,256,8,64]{1,3,2,0:T(8,128)}, f32[8,256,8]{1,2,0:T(8,128)}, /*index=5*/f3...) while((s32[]{:T(128)}, f32[8]{0:T(128)}, ...), condition=%wide.region_24.25_spmd.clone, body=%wide.region_10.0_spmd.clone.sunk | while | flops 2126610432 | bytes 15952340 | solution.py:56
  337.4 3.4 fusion.252
  411.8 3.4 fusion.252
  503.2 6.9 copy.104
  510.1 7.5 reshape.371
  517.7 11.5 %multiply_reduce_fusion.6 = (f32[512]{0:T(512)S(1)}, f32[512]{0:T(512)S(1)}, f32[512]{0:T(512)S(1)}, f32[512]{0:T(512)S(1)}, f32[512]{0:T(512)S(1)}, /*index=5*/f32[2048,512]{1,0:T(8,128)S(1)}) fusion(f32[2048,512]{1,0:T(8,128)} %copy-done, f32[2048,2,512]{2,0,1:T(8,128)} %copy-done.1, f32[2048,512]{1,0:T(8,128)} %get-tuple-element.766, ...), kind=kLoop, calls=%fused_computation.164 | loop fusion | flops 20968960 | bytes 25178112 | tf_op jit(solution)/shard_map/transpose(jvp())/reduce_sum | solution.py:19
  529.2 5.8 broadcast_multiply_fusion
  535.0 7.1 fusion.127
  542.2 8.2 fusion.107
  554.3 6.8 bitcast_add_fusion
  562.4 7.8 fusion.148
  579.6 40.8 %all-reduce.21 = bf16[2048,256]{1,0:T(8,128)(2,1)S(1)} all-reduce(f32[2048,256]{1,0:T(8,128)S(1)} %pad_add_fusion.3), channel_id=1, replica_groups=mesh['dp'=8,'tensor'=4] {'tensor'}, use_global_device_ids=true, to_apply=%region_26.27 | all-reduce | flops 524288 | bytes 3145728 | tf_op jit(solution)/shard_map/psum | solution.py:195
  620.5 4.9 fusion.162
  628.7 8.8 reduce-scatter.11.cloned.1.call-done
  639.7 71.4 %reduce-scatter.9.cloned.1.call-done = f32[512,1024]{1,0:T(8,128)} async-done(((f32[2048,1024]{1,0:T(8,128)}), f32[512,1024]{1,0:T(8,128)}) %reduce-scatter.9.cloned.1.call-update) | async-done | bytes 2097168 | tf_op jit(solution)/shard_map/reduce_scatter | solution.py:206
  713.8 41.1 %all-reduce.19 = (f32[1024]{0:T(1024)}, f32[4,2048]{1,0:T(4,128)}, f32[2048]{0:T(1024)}, f32[4,256]{1,0:T(4,128)}, f32[256]{0:T(256)}, /*index=5*/f32[32]{0:T(128)}, f32[32]{0:T(128)}, f32[32]{0:T(128)}, f32[2048]{0:T(1024)}) all-reduce(f32[1024]{0:T(1024)S(1)} %get-tuple-element.689, ...), channel_id=1, replica_groups=mesh['dp'=8,'tensor'=4] {'dp','tensor'}, use_global_device_ids=true, to_apply=%region_29.30 | all-reduce | flops 14688 | bytes 117504 | tf_op jit(solution)/shard_map/psum | solution.py:225
  754.9 30.9 %reduce-scatter.7.cloned.1.call-done = f32[512,1024]{1,0:T(8,128)} async-done(((f32[2048,1024]{1,0:T(8,128)}), f32[512,1024]{1,0:T(8,128)}) %reduce-scatter.7.cloned.1.call-update) | async-done | bytes 2097168 | tf_op jit(solution)/shard_map/reduce_scatter | solution.py:159
  785.8 4.3 fusion.122
  790.0 54.2 %reduce-scatter.15.cloned.1.call-done = f32[128,8]{0,1:T(8,128)} async-done(((f32[1024,8]{0,1:T(8,128)}), f32[128,8]{0,1:T(8,128)}) %reduce-scatter.15.cloned.1.call-update) | async-done | bytes 4112 | tf_op jit(solution)/shard_map/reduce_scatter | solution.py:222
  844.3 67.1 %reduce-scatter.13.cloned.1.call-done = f32[128,256]{1,0:T(8,128)} async-done(((f32[1024,256]{1,0:T(8,128)}), f32[128,256]{1,0:T(8,128)}) %reduce-scatter.13.cloned.1.call-update) | async-done | bytes 131088 | tf_op jit(solution)/shard_map/reduce_scatter | solution.py:221
  (599 shorter events, 297.5 us)
Async XLA Ops:
  7.2 6.4 copy-start.52
  7.2 7.1 copy-start.55
  7.2 7.2 copy-start.56
  7.2 8.9 copy-start.48
  7.2 8.9 copy-start.49
  7.2 36.9 %copy-start.20 = (bf16[128,256]{1,0:T(8,128)(2,1)S(1)}, bf16[128,256]{1,0:T(8,128)(2,1)}, u32[]{:S(2)}) copy-start(bf16[128,256]{1,0:T(8,128)(2,1)} %param.23) | copy-start | bytes 196612
  7.3 70.3 %all-gather.6.cloned.1.call-start = ((), (), s32[]{:S(2)}) async-start(), calls=%async_computation.6 | async-start | bytes 5242880 | tf_op jit(solution)/shard_map/all_gather | solution.py:128
  8.9 7.3 copy-start.36
  8.9 7.3 copy-start.24
  11.4 90.1 %all-gather.8.cloned.1.call-start = ((), (), s32[]{:S(2)}) async-start(), calls=%async_computation.7 | async-start | bytes 2359296 | tf_op jit(solution)/shard_map/all_gather | solution.py:121
  12.2 240.5 %all-gather.12.cloned.1.call-start = ((), (), s32[]{:S(2)}) async-start(), calls=%async_computation.15 | async-start | bytes 5242880 | tf_op jit(solution)/shard_map/all_gather | solution.py:167
  13.0 247.0 %all-gather.10.cloned.1.call-start = ((), (), s32[]{:S(2)}) async-start(), calls=%async_computation.8 | async-start | bytes 1179648 | tf_op jit(solution)/shard_map/all_gather | solution.py:124
  13.6 613.3 %reduce-scatter.17.cloned.1.call-start = ((), (), s32[]{:S(2)}) async-start(), calls=%async_computation.14 | async-start | bytes 2359296 | tf_op jit(solution)/shard_map/reduce_scatter | solution.py:223
  15.2 259.0 %copy-start.26 = (f32[512]{0:T(512)}, f32[512]{0:T(512)S(1)}, u32[]{:S(2)}) copy-start(f32[512]{0:T(512)S(1)} %dynamic_slice.100) | copy-start | bytes 6148
  16.1 258.1 %copy-start.22 = (f32[512]{0:T(512)}, f32[512]{0:T(512)S(1)}, u32[]{:S(2)}) copy-start(f32[512]{0:T(512)S(1)} %mul.863) | copy-start | bytes 6148
  16.2 65.2 %copy-start.39 = (f32[1,256]{1,0:T(1,128)}, f32[1,256]{1,0:T(1,128)S(1)}, u32[]{:S(2)}) copy-start(f32[1,256]{1,0:T(1,128)S(1)} %get-tuple-element.793) | copy-start | bytes 3076
  16.2 65.2 %copy-start.41 = (f32[1,256]{1,0:T(1,128)}, f32[1,256]{1,0:T(1,128)S(1)}, u32[]{:S(2)}) copy-start(f32[1,256]{1,0:T(1,128)S(1)} %get-tuple-element.794) | copy-start | bytes 3076
  16.2 65.2 %copy-start.43 = (f32[1,256]{1,0:T(1,128)}, f32[1,256]{1,0:T(1,128)S(1)}, u32[]{:S(2)}) copy-start(f32[1,256]{1,0:T(1,128)S(1)} %get-tuple-element.795) | copy-start | bytes 3076
  16.2 65.2 %copy-start.45 = (f32[1,256]{1,0:T(1,128)}, f32[1,256]{1,0:T(1,128)S(1)}, u32[]{:S(2)}) copy-start(f32[1,256]{1,0:T(1,128)S(1)} %get-tuple-element.796) | copy-start | bytes 3076
  44.1 86.8 %copy-start.18 = (bf16[1024,8]{0,1:T(8,128)(2,1)}, bf16[1024,8]{0,1:T(8,128)(2,1)S(1)}, u32[]{:S(2)}) copy-start(bf16[1024,8]{0,1:T(8,128)(2,1)S(1)} %all_gather.19) | copy-start | bytes 49156
  44.2 37.3 %copy-start.51 = (f32[256]{0:T(256)S(1)}, f32[256]{0:T(256)}, u32[]{:S(2)}) copy-start(f32[256]{0:T(256)} %param.29) | copy-start | bytes 3076
  76.6 4.8 copy-start.10
  77.5 34.7 %copy-start.28 = (f32[1,512]{1,0:T(1,128)}, f32[1,512]{1,0:T(1,128)S(1)}, u32[]{:S(2)}) copy-start(f32[1,512]{1,0:T(1,128)S(1)} %get-tuple-element.787) | copy-start | bytes 6148
  77.5 34.7 %copy-start.30 = (f32[1,512]{1,0:T(1,128)}, f32[1,512]{1,0:T(1,128)S(1)}, u32[]{:S(2)}) copy-start(f32[1,512]{1,0:T(1,128)S(1)} %get-tuple-element.788) | copy-start | bytes 6148
  77.6 34.7 %copy-start.32 = (f32[1,512]{1,0:T(1,128)}, f32[1,512]{1,0:T(1,128)S(1)}, u32[]{:S(2)}) copy-start(f32[1,512]{1,0:T(1,128)S(1)} %get-tuple-element.789) | copy-start | bytes 6148
  77.6 34.7 %copy-start.34 = (f32[1,512]{1,0:T(1,128)}, f32[1,512]{1,0:T(1,128)S(1)}, u32[]{:S(2)}) copy-start(f32[1,512]{1,0:T(1,128)S(1)} %get-tuple-element.790) | copy-start | bytes 6148
  112.3 4.7 copy-start
  252.7 21.6 %copy-start.16 = (f32[2048]{0:T(1024)}, f32[2048]{0:T(1024)S(1)}, u32[]{:S(2)}) copy-start(f32[2048]{0:T(1024)S(1)} %get-tuple-element.792) | copy-start | bytes 24580
  260.0 377.4 %reduce-scatter.11.cloned.1.call-start = ((), (), s32[]{:S(2)}) async-start(), calls=%async_computation.11 | async-start | bytes 4718592 | tf_op jit(solution)/shard_map/reduce_scatter | solution.py:220
  510.1 7.5 copy-start.23
  517.6 11.6 %copy-start.29 = (f32[1,512]{1,0:T(1,128)S(1)}, f32[1,512]{1,0:T(1,128)}, u32[]{:S(2)}) copy-start(f32[1,512]{1,0:T(1,128)} %copy-done.28) | copy-start | bytes 6148
  517.6 11.6 %copy-start.31 = (f32[1,512]{1,0:T(1,128)S(1)}, f32[1,512]{1,0:T(1,128)}, u32[]{:S(2)}) copy-start(f32[1,512]{1,0:T(1,128)} %copy-done.30) | copy-start | bytes 6148
  517.6 11.6 %copy-start.33 = (f32[1,512]{1,0:T(1,128)S(1)}, f32[1,512]{1,0:T(1,128)}, u32[]{:S(2)}) copy-start(f32[1,512]{1,0:T(1,128)} %copy-done.32) | copy-start | bytes 6148
  517.6 11.6 %copy-start.35 = (f32[1,512]{1,0:T(1,128)S(1)}, f32[1,512]{1,0:T(1,128)}, u32[]{:S(2)}) copy-start(f32[1,512]{1,0:T(1,128)} %copy-done.34) | copy-start | bytes 6148
  535.0 7.2 copy-start.2
  550.4 160.6 %reduce-scatter.9.cloned.1.call-start = ((), (), s32[]{:S(2)}) async-start(), calls=%async_computation.10 | async-start | bytes 10485760 | tf_op jit(solution)/shard_map/reduce_scatter | solution.py:206
  561.2 224.6 %reduce-scatter.7.cloned.1.call-start = ((), (), s32[]{:S(2)}) async-start(), calls=%async_computation.9 | async-start | bytes 10485760 | tf_op jit(solution)/shard_map/reduce_scatter | solution.py:159
  570.2 274.0 %reduce-scatter.15.cloned.1.call-start = ((), (), s32[]{:S(2)}) async-start(), calls=%async_computation.13 | async-start | bytes 36864 | tf_op jit(solution)/shard_map/reduce_scatter | solution.py:222
  620.4 5.1 copy-start.11
  620.4 5.1 copy-start.47
  620.4 5.1 copy-start.50
  620.4 6.2 copy-start.38
  620.4 6.2 copy-start.53
  620.4 90.6 %copy-start.4 = (bf16[1,512,1024]{2,1,0:T(8,128)(2,1)S(1)}, bf16[1,512,1024]{2,1,0:T(8,128)(2,1)}, u32[]{:S(2)}) copy-start(bf16[1,512,1024]{2,1,0:T(8,128)(2,1)} %param.19) | copy-start | bytes 3145732
  620.5 90.6 %copy-start.21 = (f32[1024]{0:T(1024)S(1)}, f32[1024]{0:T(1024)}, u32[]{:S(2)}) copy-start(f32[1024]{0:T(1024)} %param.21) | copy-start | bytes 12292
  620.5 90.6 %copy-start.25 = (f32[512]{0:T(512)S(1)}, f32[512]{0:T(512)}, u32[]{:S(2)}) copy-start(f32[512]{0:T(512)} %copy-done.24) | copy-start | bytes 6148
  620.5 290.9 %reduce-scatter.13.cloned.1.call-start = ((), (), s32[]{:S(2)}) async-start(), calls=%async_computation.12 | async-start | bytes 1179648 | tf_op jit(solution)/shard_map/reduce_scatter | solution.py:221
  625.4 129.5 %copy-start.37 = (f32[512]{0:T(512)S(1)}, f32[512]{0:T(512)}, u32[]{:S(2)}) copy-start(f32[512]{0:T(512)} %copy-done.36) | copy-start | bytes 6148
  (19 other events, 43.6 us)
Sparse Core Ops, SparseCore 0:
  11.6 37.1 all-gather.5
  51.5 49.9 all-gather.7
  103.1 32.9 all-gather.11
  138.1 40.3 all-gather.9
  260.1 68.2 reduce-scatter.16
  550.6 86.8 reduce-scatter.10
  640.0 71.0 reduce-scatter.8
  713.6 72.0 reduce-scatter.6
  789.5 54.7 reduce-scatter.14
  848.1 63.1 reduce-scatter.12
where the time goes:
time: 926 us; the launch traced here: 919 us
  waiting for transfers between devices  249 us (27%)
  matrix products  235 us (25%)
  blocking collectives  155 us (17%)
  other arithmetic  140 us (15%)
  local copies, waits for them, and re-layouts  123 us (13%)
  between operations  15.3 us (2%)
    dot_general x24, matrix products, step_block(): jnp.einsum('ijh,jhp->ihp', weights, x_block, precision=FULL_PRECISION)  78.3 us
    reduce_scatter x1, waiting for transfers between devices, body(): lax.psum_scatter(from_zx + lax.dot_general(grad_dt_low, dt_full, CONTRACT...  71.4 us
    reduce_scatter x1, waiting for transfers between devices, body(): lax.psum_scatter(grad_bc_w, 'dp', scatter_dimension=0, tiled=True)  67.1 us
    reduce_scatter x1, waiting for transfers between devices, body(): lax.psum_scatter(grad_dt_w, 'dp', scatter_dimension=0, tiled=True)  54.2 us
    psum x1, blocking collectives, body(): lax.psum((grad_norm_gain, widen(grad_x_taps, chan_start, total_channels),...  41.1 us
    psum x1, blocking collectives, body(): grad_bc_in = lax.psum(grad_bc_part, 'tensor').astype(jnp.bfloat16)  40.8 us
    another operation x73, other arithmetic  39.1 us
    dot_general x32, matrix products, step_block(): jnp.einsum('in,hpn->ihp', c_block, state, precision=FULL_PRECISION)  35.8 us
  transfers between devices with their start and end apart: 10, of which 6 were waited for; matrix products, arithmetic and copies ran while one was open for 53% of the time, Pallas kernels for 0%

commit v1 on v0

--- a/solution.py
+++ b/solution.py
@@ -192,7 +192,7 @@
     grad_x_in, grad_bc_part, grad_x_taps, grad_x_shift, grad_bc_taps, grad_bc_shift = conv_back(
         (grad_x_low, jnp.concatenate([grad_b, grad_c], axis=1))
     )
-    grad_bc_in = lax.psum(grad_bc_part, "tensor").astype(jnp.bfloat16)
+    grad_bc_in = jnp.sum(lax.all_gather(grad_bc_part, "tensor"), axis=0).astype(jnp.bfloat16)
     grad_zx = jnp.stack([grad_gate_in.astype(jnp.bfloat16), grad_x_in.astype(jnp.bfloat16)], axis=1)
     grad_dt_low = grad_dt_in.astype(jnp.bfloat16)
     grad_zx_w = jnp.einsum("ld,lkc->dkc", hidden, grad_zx, preferred_element_type=jnp.float32)

time: 926 us -> 1010 us (1.091)
  waiting for transfers between devices: 249 us -> 370 us
  blocking collectives: 155 us -> 114 us
    reduce_scatter x1, waiting for transfers between devices: 8.77 us -> 89.3 us  [body(): lax.psum_scatter(grad_zx_w, 'dp', scatter_dimension=0, tiled=True)]
    psum x1 -> x0, blocking collectives: 40.8 us -> none  [body(): grad_bc_in = lax.psum(grad_bc_part, 'tensor').astype(jnp.bfloat16)]
    reduce_scatter x1, waiting for transfers between devices: 0.01 us -> 40.1 us  [body(): lax.psum_scatter(grad_out_w, 'dp', scatter_dimension=0, tiled=True)]
    unnamed x119 -> x113, local copies, waits for them, and re-layouts: 28.6 us -> 24.6 us
  transfers between devices with their start and end apart: 10 -> 11, of which waited for: 6 -> 7; matrix products, arithmetic and copies ran while one was open for 53% -> 25% of each run, Pallas kernels for 0% -> 0%
where the time goes in v1:
time: 1010 us
  waiting for transfers between devices  370 us (37%)
  matrix products  237 us (23%)
  other arithmetic  148 us (15%)
  local copies, waits for them, and re-layouts  119 us (12%)
  blocking collectives  114 us (11%)
  between operations  14.8 us (1%)
    reduce_scatter x1, waiting for transfers between devices, body(): lax.psum_scatter(grad_zx_w, 'dp', scatter_dimension=0, tiled=True)  89.3 us
    dot_general x24, matrix products, step_block(): jnp.einsum('ijh,jhp->ihp', weights, x_block, precision=FULL_PRECISION)  78.3 us
    reduce_scatter x1, waiting for transfers between devices, body(): lax.psum_scatter(from_zx + lax.dot_general(grad_dt_low, dt_full, CONTRACT...  71.4 us
    reduce_scatter x1, waiting for transfers between devices, body(): lax.psum_scatter(grad_bc_w, 'dp', scatter_dimension=0, tiled=True)  67.3 us
    reduce_scatter x1, waiting for transfers between devices, body(): lax.psum_scatter(grad_dt_w, 'dp', scatter_dimension=0, tiled=True)  54.1 us
    psum x1, blocking collectives, body(): lax.psum((grad_norm_gain, widen(grad_x_taps, chan_start, total_channels),...  41.2 us
    reduce_scatter x1, waiting for transfers between devices, body(): lax.psum_scatter(grad_out_w, 'dp', scatter_dimension=0, tiled=True)  40.1 us
    another operation x73, other arithmetic  39.1 us
  transfers between devices with their start and end apart: 11, of which 7 were waited for; matrix products, arithmetic and copies ran while one was open for 25% of the time, Pallas kernels for 0%

profile of v1, /device:TPU:0, one launch (start us, length us, event | category | flops | bytes accessed | tf_op | source)
XLA Modules:
  0.0 1005.0 jit_solution(12777710000781962726)
XLA Ops:
  16.2 27.9 %all_gather.25 = bf16[1024,8]{0,1:T(8,128)(2,1)S(1)} all-gather(bf16[128,8]{0,1:T(8,128)(2,1)S(1)} %copy-done.46), channel_id=1, replica_groups=mesh['dp'=8,'tensor'=4] {'dp'}, dimensions={0}, use_global_device_ids=true | all-gather | bytes 18432 | tf_op jit(solution)/shard_map/all_gather | solution.py:123
  44.2 32.4 %all_gather.27 = bf16[1024,256]{1,0:T(8,128)(2,1)S(1)} all-gather(bf16[128,256]{1,0:T(8,128)(2,1)S(1)} %copy-done.17), channel_id=1, replica_groups=mesh['dp'=8,'tensor'=4] {'dp'}, dimensions={0}, use_global_device_ids=true | all-gather | bytes 589824 | tf_op jit(solution)/shard_map/all_gather | solution.py:122
  77.6 3.8 fusion.161
  86.3 15.2 %all-gather.10.cloned.1.call-done = bf16[1024,2,512]{2,0,1:T(8,128)(2,1)} async-done(((bf16[128,2,512]{2,0,1:T(8,128)(2,1)}), bf16[1024,2,512]{2,0,1:T(8,128)(2,1)}) %all-gather.10.cloned.1.call-update) | async-done | bytes 2097168 | tf_op jit(solution)/shard_map/all_gather | solution.py:121
  101.5 7.1 fusion.109
  111.8 4.7 fusion.123
  116.5 7.1 reshape.373
  123.6 6.8 copy.89
  130.4 4.0 compare_select_fusion.2
  136.9 87.5 %while.43 = (s32[]{:T(128)}, f32[8,64,128]{2,1,0:T(8,128)S(1)}, f32[8,256,8,64]{1,3,2,0:T(8,128)}, f32[8,8,64,128]{3,2,1,0:T(8,128)}, f32[8,256,8]{1,2,0:T(8,128...) while((s32[]{:T(128)}, f32[8,64,128]{2,1,0:T(8,128)S(1)}, ...), condition=%wide.region_4.5_spmd.clone.clone, body=%wide.region_1.4_spmd.clone.clone.sunk | while | flops 909711360 | bytes 5641051 | solution.py:56
  139.5 3.6 fusion.270
  150.5 3.6 fusion.270
  161.4 3.6 fusion.270
  172.3 3.6 fusion.270
  183.2 3.6 fusion.270
  194.2 3.6 fusion.270
  205.1 3.6 fusion.270
  216.0 3.6 fusion.270
  224.4 6.9 copy.101
  231.3 7.5 reshape.370
  238.8 7.4 multiply_reduce_fusion.8
  246.2 5.7 psum.77
  252.1 7.4 fusion.96
  259.5 6.7 psum.78
  266.2 11.4 %multiply_reduce_fusion.3 = (f32[512]{0:T(512)}, f32[2048,512]{1,0:T(8,128)}, bf16[2048,1,512]{2,0,1:T(8,128)(2,1)}) fusion(f32[2048,512]{1,0:T(8,128)} %get-tuple-element.766, f32[2048,2,512]{2,0,1:T(8,128)} %copy-done.1, f32[2048]{0:T(1024)S(1)} %broadcast_multiply_fusion.8, f32[2048,512]{1,0:T(8,128)} %get-tuple-element.762, ...), kind=kLoop, calls=%fused_computation.161 | loop fusion | flops 30408192 | bytes 25196544 | tf_op jit(solution)/shard_map/transpose(jvp())/reduce_sum | solution.py:83
  277.7 7.0 reshape.371
  284.7 6.8 copy.94
  296.8 198.2 %while.42 = (s32[]{:T(128)}, f32[8]{0:T(128)}, f32[8,64,128]{2,1,0:T(8,128)S(1)}, f32[8,256,8,64]{1,3,2,0:T(8,128)}, f32[8,256,8]{1,2,0:T(8,128)}, /*index=5*/f3...) while((s32[]{:T(128)}, f32[8]{0:T(128)}, ...), condition=%wide.region_24.25_spmd.clone, body=%wide.region_10.0_spmd.clone.sunk | while | flops 2126610432 | bytes 15952340 | solution.py:56
  495.0 6.2 multiply_reduce_fusion.12
  503.9 7.3 fusion.130
  511.3 7.2 copy.104
  518.4 7.5 reshape.372
  526.0 11.5 %multiply_reduce_fusion.6 = (f32[512]{0:T(512)S(1)}, f32[512]{0:T(512)S(1)}, f32[512]{0:T(512)S(1)}, f32[512]{0:T(512)S(1)}, f32[512]{0:T(512)S(1)}, /*index=5*/f32[2048,512]{1,0:T(8,128)S(1)}) fusion(f32[2048,512]{1,0:T(8,128)} %copy-done, f32[2048,2,512]{2,0,1:T(8,128)} %copy-done.1, f32[2048,512]{1,0:T(8,128)} %get-tuple-element.766, ...), kind=kLoop, calls=%fused_computation.164 | loop fusion | flops 20968960 | bytes 25178112 | tf_op jit(solution)/shard_map/transpose(jvp())/reduce_sum | solution.py:19
  537.5 5.8 broadcast_multiply_fusion
  543.3 7.1 fusion.127
  550.5 8.3 fusion.107
  562.7 6.8 bitcast_add_fusion
  570.7 7.8 fusion.148
  582.2 4.4 reduce_sum.410
  586.7 5.0 fusion.162
  593.1 40.1 %reduce-scatter.17.cloned.1.call-done = f32[128,512]{0,1:T(8,128)} async-done(((f32[1024,512]{0,1:T(8,128)}), f32[128,512]{0,1:T(8,128)}) %reduce-scatter.17.cloned.1.call-update) | async-done | bytes 262160 | tf_op jit(solution)/shard_map/reduce_scatter | solution.py:223
  634.9 89.3 %reduce-scatter.11.cloned.1.call-done = f32[128,2,512]{2,0,1:T(8,128)} async-done(((f32[1024,2,512]{2,0,1:T(8,128)}), f32[128,2,512]{2,0,1:T(8,128)}) %reduce-scatter.11.cloned.1.call-update) | async-done | bytes 524304 | tf_op jit(solution)/shard_map/reduce_scatter | solution.py:220
  726.5 71.4 %reduce-scatter.9.cloned.1.call-done = f32[512,1024]{1,0:T(8,128)} async-done(((f32[2048,1024]{1,0:T(8,128)}), f32[512,1024]{1,0:T(8,128)}) %reduce-scatter.9.cloned.1.call-update) | async-done | bytes 2097168 | tf_op jit(solution)/shard_map/reduce_scatter | solution.py:206
  800.6 41.2 %all-reduce.19 = (f32[1024]{0:T(1024)}, f32[4,2048]{1,0:T(4,128)}, f32[2048]{0:T(1024)}, f32[4,256]{1,0:T(4,128)}, f32[256]{0:T(256)}, /*index=5*/f32[32]{0:T(128)}, f32[32]{0:T(128)}, f32[32]{0:T(128)}, f32[2048]{0:T(1024)}) all-reduce(f32[1024]{0:T(1024)S(1)} %get-tuple-element.689, ...), channel_id=1, replica_groups=mesh['dp'=8,'tensor'=4] {'dp','tensor'}, use_global_device_ids=true, to_apply=%region_29.30 | all-reduce | flops 14688 | bytes 117504 | tf_op jit(solution)/shard_map/psum | solution.py:225
  841.8 30.9 %reduce-scatter.7.cloned.1.call-done = f32[512,1024]{1,0:T(8,128)} async-done(((f32[2048,1024]{1,0:T(8,128)}), f32[512,1024]{1,0:T(8,128)}) %reduce-scatter.7.cloned.1.call-update) | async-done | bytes 2097168 | tf_op jit(solution)/shard_map/reduce_scatter | solution.py:159
  872.7 4.3 fusion.122
  876.9 54.1 %reduce-scatter.15.cloned.1.call-done = f32[128,8]{0,1:T(8,128)} async-done(((f32[1024,8]{0,1:T(8,128)}), f32[128,8]{0,1:T(8,128)}) %reduce-scatter.15.cloned.1.call-update) | async-done | bytes 4112 | tf_op jit(solution)/shard_map/reduce_scatter | solution.py:222
  931.0 67.3 %reduce-scatter.13.cloned.1.call-done = f32[128,256]{1,0:T(8,128)} async-done(((f32[1024,256]{1,0:T(8,128)}), f32[128,256]{1,0:T(8,128)}) %reduce-scatter.13.cloned.1.call-update) | async-done | bytes 131088 | tf_op jit(solution)/shard_map/reduce_scatter | solution.py:221
  (596 shorter events, 300.8 us)
Async XLA Ops:
  7.2 6.4 copy-start.49
  7.2 7.1 copy-start.52
  7.2 7.2 copy-start.53
  7.2 8.9 copy-start.45
  7.2 8.9 copy-start.46
  7.2 36.9 %copy-start.17 = (bf16[128,256]{1,0:T(8,128)(2,1)S(1)}, bf16[128,256]{1,0:T(8,128)(2,1)}, u32[]{:S(2)}) copy-start(bf16[128,256]{1,0:T(8,128)(2,1)} %param.23) | copy-start | bytes 196612
  7.3 70.3 %all-gather.8.cloned.1.call-start = ((), (), s32[]{:S(2)}) async-start(), calls=%async_computation.6 | async-start | bytes 5242880 | tf_op jit(solution)/shard_map/all_gather | solution.py:128
  8.9 7.3 copy-start.33
  8.9 7.3 copy-start.21
  11.4 90.1 %all-gather.10.cloned.1.call-start = ((), (), s32[]{:S(2)}) async-start(), calls=%async_computation.7 | async-start | bytes 2359296 | tf_op jit(solution)/shard_map/all_gather | solution.py:121
  12.2 239.8 %all-gather.12.cloned.1.call-start = ((), (), s32[]{:S(2)}) async-start(), calls=%async_computation.8 | async-start | bytes 1179648 | tf_op jit(solution)/shard_map/all_gather | solution.py:124
  13.0 239.1 %all-gather.14.cloned.1.call-start = ((), (), s32[]{:S(2)}) async-start(), calls=%async_computation.15 | async-start | bytes 5242880 | tf_op jit(solution)/shard_map/all_gather | solution.py:167
  13.6 568.6 %all-gather.16.cloned.1.call-start = ((), (), s32[]{:S(2)}) async-start(), calls=%async_computation.16 | async-start | bytes 10485760 | tf_op jit(solution)/shard_map/all_gather | solution.py:195
  15.2 251.0 %copy-start.23 = (f32[512]{0:T(512)}, f32[512]{0:T(512)S(1)}, u32[]{:S(2)}) copy-start(f32[512]{0:T(512)S(1)} %dynamic_slice.100) | copy-start | bytes 6148
  16.1 250.1 %copy-start.19 = (f32[512]{0:T(512)}, f32[512]{0:T(512)S(1)}, u32[]{:S(2)}) copy-start(f32[512]{0:T(512)S(1)} %mul.863) | copy-start | bytes 6148
  16.2 65.2 %copy-start.36 = (f32[1,256]{1,0:T(1,128)}, f32[1,256]{1,0:T(1,128)S(1)}, u32[]{:S(2)}) copy-start(f32[1,256]{1,0:T(1,128)S(1)} %get-tuple-element.793) | copy-start | bytes 3076
  16.2 65.2 %copy-start.38 = (f32[1,256]{1,0:T(1,128)}, f32[1,256]{1,0:T(1,128)S(1)}, u32[]{:S(2)}) copy-start(f32[1,256]{1,0:T(1,128)S(1)} %get-tuple-element.794) | copy-start | bytes 3076
  16.2 65.2 %copy-start.40 = (f32[1,256]{1,0:T(1,128)}, f32[1,256]{1,0:T(1,128)S(1)}, u32[]{:S(2)}) copy-start(f32[1,256]{1,0:T(1,128)S(1)} %get-tuple-element.795) | copy-start | bytes 3076
  16.2 65.2 %copy-start.42 = (f32[1,256]{1,0:T(1,128)}, f32[1,256]{1,0:T(1,128)S(1)}, u32[]{:S(2)}) copy-start(f32[1,256]{1,0:T(1,128)S(1)} %get-tuple-element.796) | copy-start | bytes 3076
  44.1 86.3 %copy-start.15 = (bf16[1024,8]{0,1:T(8,128)(2,1)}, bf16[1024,8]{0,1:T(8,128)(2,1)S(1)}, u32[]{:S(2)}) copy-start(bf16[1024,8]{0,1:T(8,128)(2,1)S(1)} %all_gather.25) | copy-start | bytes 49156
  44.1 37.3 %copy-start.48 = (f32[256]{0:T(256)S(1)}, f32[256]{0:T(256)}, u32[]{:S(2)}) copy-start(f32[256]{0:T(256)} %param.29) | copy-start | bytes 3076
  77.5 34.3 %copy-start.25 = (f32[1,512]{1,0:T(1,128)}, f32[1,512]{1,0:T(1,128)S(1)}, u32[]{:S(2)}) copy-start(f32[1,512]{1,0:T(1,128)S(1)} %get-tuple-element.787) | copy-start | bytes 6148
  77.5 34.3 %copy-start.27 = (f32[1,512]{1,0:T(1,128)}, f32[1,512]{1,0:T(1,128)S(1)}, u32[]{:S(2)}) copy-start(f32[1,512]{1,0:T(1,128)S(1)} %get-tuple-element.788) | copy-start | bytes 6148
  77.6 34.2 %copy-start.29 = (f32[1,512]{1,0:T(1,128)}, f32[1,512]{1,0:T(1,128)S(1)}, u32[]{:S(2)}) copy-start(f32[1,512]{1,0:T(1,128)S(1)} %get-tuple-element.789) | copy-start | bytes 6148
  77.6 34.2 %copy-start.31 = (f32[1,512]{1,0:T(1,128)}, f32[1,512]{1,0:T(1,128)S(1)}, u32[]{:S(2)}) copy-start(f32[1,512]{1,0:T(1,128)S(1)} %get-tuple-element.790) | copy-start | bytes 6148
  252.0 14.2 %copy-start.13 = (f32[2048]{0:T(1024)}, f32[2048]{0:T(1024)S(1)}, u32[]{:S(2)}) copy-start(f32[2048]{0:T(1024)S(1)} %get-tuple-element.792) | copy-start | bytes 24580
  495.0 6.3 copy-start.37
  495.0 6.3 copy-start.39
  495.0 6.3 copy-start.41
  495.0 6.3 copy-start.43
  503.9 129.3 %reduce-scatter.17.cloned.1.call-start = ((), (), s32[]{:S(2)}) async-start(), calls=%async_computation.14 | async-start | bytes 2359296 | tf_op jit(solution)/shard_map/reduce_scatter | solution.py:223
  511.2 213.0 %reduce-scatter.11.cloned.1.call-start = ((), (), s32[]{:S(2)}) async-start(), calls=%async_computation.11 | async-start | bytes 4718592 | tf_op jit(solution)/shard_map/reduce_scatter | solution.py:220
  518.4 7.5 copy-start.20
  525.9 11.5 %copy-start.26 = (f32[1,512]{1,0:T(1,128)S(1)}, f32[1,512]{1,0:T(1,128)}, u32[]{:S(2)}) copy-start(f32[1,512]{1,0:T(1,128)} %copy-done.25) | copy-start | bytes 6148
  525.9 11.5 %copy-start.28 = (f32[1,512]{1,0:T(1,128)S(1)}, f32[1,512]{1,0:T(1,128)}, u32[]{:S(2)}) copy-start(f32[1,512]{1,0:T(1,128)} %copy-done.27) | copy-start | bytes 6148
  525.9 11.5 %copy-start.30 = (f32[1,512]{1,0:T(1,128)S(1)}, f32[1,512]{1,0:T(1,128)}, u32[]{:S(2)}) copy-start(f32[1,512]{1,0:T(1,128)} %copy-done.29) | copy-start | bytes 6148
  525.9 11.5 %copy-start.32 = (f32[1,512]{1,0:T(1,128)S(1)}, f32[1,512]{1,0:T(1,128)}, u32[]{:S(2)}) copy-start(f32[1,512]{1,0:T(1,128)} %copy-done.31) | copy-start | bytes 6148
  543.3 7.2 copy-start.2
  558.8 239.1 %reduce-scatter.9.cloned.1.call-start = ((), (), s32[]{:S(2)}) async-start(), calls=%async_computation.10 | async-start | bytes 10485760 | tf_op jit(solution)/shard_map/reduce_scatter | solution.py:206
  569.5 303.1 %reduce-scatter.7.cloned.1.call-start = ((), (), s32[]{:S(2)}) async-start(), calls=%async_computation.9 | async-start | bytes 10485760 | tf_op jit(solution)/shard_map/reduce_scatter | solution.py:159
  578.6 352.4 %reduce-scatter.15.cloned.1.call-start = ((), (), s32[]{:S(2)}) async-start(), calls=%async_computation.13 | async-start | bytes 36864 | tf_op jit(solution)/shard_map/reduce_scatter | solution.py:222
  582.1 416.2 %reduce-scatter.13.cloned.1.call-start = ((), (), s32[]{:S(2)}) async-start(), calls=%async_computation.12 | async-start | bytes 1179648 | tf_op jit(solution)/shard_map/reduce_scatter | solution.py:221
  586.6 6.3 copy-start.35
  586.6 6.3 copy-start.50
  586.6 211.3 %copy-start.3 = (bf16[1,512,1024]{2,1,0:T(8,128)(2,1)S(1)}, bf16[1,512,1024]{2,1,0:T(8,128)(2,1)}, u32[]{:S(2)}) copy-start(bf16[1,512,1024]{2,1,0:T(8,128)(2,1)} %param.19) | copy-start | bytes 3145732
  586.6 211.3 %copy-start.18 = (f32[1024]{0:T(1024)S(1)}, f32[1024]{0:T(1024)}, u32[]{:S(2)}) copy-start(f32[1024]{0:T(1024)} %param.21) | copy-start | bytes 12292
  586.7 211.3 %copy-start.22 = (f32[512]{0:T(512)S(1)}, f32[512]{0:T(512)}, u32[]{:S(2)}) copy-start(f32[512]{0:T(512)} %copy-done.21) | copy-start | bytes 6148
  591.6 250.2 %copy-start.34 = (f32[512]{0:T(512)S(1)}, f32[512]{0:T(512)}, u32[]{:S(2)}) copy-start(f32[512]{0:T(512)} %copy-done.33) | copy-start | bytes 6148
  (17 other events, 50.9 us)
Sparse Core Ops, SparseCore 0:
  11.6 37.1 all-gather.7
  51.5 49.9 all-gather.9
  103.6 38.7 all-gather.11
  143.9 33.0 all-gather.13
  504.0 56.4 all-gather.15
  563.8 69.2 reduce-scatter.16
  636.7 87.4 reduce-scatter.10
  726.8 71.0 reduce-scatter.8
  800.5 72.1 reduce-scatter.6
  876.2 54.7 reduce-scatter.14
  935.0 63.2 reduce-scatter.12
